TPU v7x, 128 devices: a whole 4x4x4 slice. The times are simulated.
128 devices in a mesh: grp: 4 (over z), dev: 32 (over x, y, core).
Axes of the slice: x: 4, y: 4, z: 4, core: 2. Of those that a mesh axis runs over, the one named last changes fastest.
Arguments:
- qkv_weight: bfloat16 [2, 4608, 8192], P(None, ('grp', 'dev')), may hold values from -0.09375 to 0.09375
- gate_up_weight: bfloat16 [2, 4608, 73728], P(None, ('grp', 'dev')), may hold values from -0.09375 to 0.09375
- head_slot: int32 [64], replicated, may hold values from 0 to 63, each once
- layer_ids: int32 [2], replicated, may hold values from 0 to 45
- stored_qkv: int32 [46, 64], replicated, may hold values from -16384 to 16383
- stored_gate_up: int32 [46, 576], replicated, may hold values from -16384 to 16383
Outputs:
- served_qkv: bfloat16 [2, 4608, 8192], P(None, 'grp', 'dev')
- served_gate_up: bfloat16 [2, 4608, 73728], P(None, 'grp', 'dev')
- qkv_mismatch: float32 [2, 64], P(None, 'dev')
- gate_up_mismatch: float32 [2, 576], P(None, 'dev')
Inputs may be any that keep to these rules, and one draw needn't show every extreme that they name: `head_slot`: each of the 64 heads appears once.
All inputs are finite; a program needn't handle non-finite values.
Results may differ from a plain program's by a relative error of at most 0.0004.
Values may be sent and summed in bfloat16 or wider, within the bound.
A program may use at most 128 MiB of HBM per device.

v0:
```python
import jax
import jax.numpy as jnp
from jax import lax
from jax.sharding import PartitionSpec as P

HEAD_DIM = 128
FF = 36864
STORED = 46
BLK = 128
NHEAD = 64


stored_unit = 1.0 / 1024.0


def cut_along(x, dim, length):
    dims = x.shape
    blocks = x.reshape(*dims[:dim], length, dims[dim] // length, *dims[dim + 1 :])
    return jnp.moveaxis(blocks, dim, 0)


def piece_ends(length, count):
    hop = length // count
    if hop >= 8:
        hop -= hop % 8
    return [hop * k for k in range(1, count)]


def in_order(blocks, dim):
    dims = list(blocks.shape[1:])
    dims[dim] *= blocks.shape[0]
    return jnp.moveaxis(blocks, 0, dim).reshape(dims)


def several_exchanges(x, axis, pieces, split_dim, concat_dim):
    blocks = cut_along(x, split_dim, lax.axis_size(axis))
    split_at = max(range(1, max(2, blocks.ndim - 1)), key=lambda d: blocks.shape[d])
    outs = []
    for piece in jnp.split(blocks, piece_ends(blocks.shape[split_at], pieces), axis=split_at):
        if piece.size:
            outs.append(lax.all_to_all(piece, axis, split_axis=0, concat_axis=0, tiled=True))
    return in_order(jnp.concatenate(outs, axis=split_at), concat_dim)


def copy_for_each(x, axis):
    copies = jnp.broadcast_to(x, (lax.axis_size(axis), *x.shape))
    return lax.all_to_all(copies, axis, split_axis=0, concat_axis=0, tiled=True)


def taken_together(x, axis):
    everything = copy_for_each(x, axis)
    return jnp.sum(everything, axis=0)


def packed_total(arrays, axis):
    ends = [0]
    for a in arrays:
        ends.append(ends[-1] + a.size)
    total = taken_together(jnp.concatenate([a.ravel() for a in arrays]), axis)
    return tuple((total[b:e].reshape(a.shape) for a, b, e in zip(arrays, ends, ends[1:])))


def finish(pieces):
    qkv_piece, gate_piece = pieces
    count = qkv_piece.shape[0]
    height = qkv_piece.shape[1]
    served_qkv = qkv_piece.reshape(count, height, qkv_piece.shape[4])
    served_gate = gate_piece.reshape(count, height, 2 * gate_piece.shape[4])
    head_local = jnp.sum(
        served_qkv.astype(jnp.float32).reshape(count, height, -1, HEAD_DIM), axis=(1, 3)
    )
    block_local = jnp.sum(
        served_gate.astype(jnp.float32).reshape(count, height, -1, BLK), axis=(1, 3)
    )
    return (served_qkv, served_gate, head_local, block_local)


def body(qkv_weight, gate_up_weight, head_slot, layer_ids, stored_qkv, stored_gate_up):
    owners = lax.axis_size("dev")
    owner = lax.axis_index("dev")
    layers = qkv_weight.shape[0]
    rows = qkv_weight.shape[1]
    slots = NHEAD // owners
    width = FF // owners
    blocks = width // BLK
    ordered = qkv_weight.reshape(layers, rows, NHEAD, HEAD_DIM)[:, :, head_slot, :]
    qkv_split = ordered.reshape(layers, rows, 1, owners, slots * HEAD_DIM)
    gate_split = gate_up_weight.reshape(layers, rows, 2, owners, width)
    moved = (
        several_exchanges(qkv_split, "dev", 2, 3, 1),
        several_exchanges(gate_split, "dev", 2, 3, 1),
    )
    results = finish(moved)
    served_qkv = results[0]
    served_gate = results[1]
    head_sum, block_sum = packed_total((results[2], results[3]), "grp")
    layer_pick = (layer_ids[:, None] == jnp.arange(STORED, dtype=jnp.int32)[None, :]).astype(
        jnp.float32
    )
    picked_qkv = jnp.dot(
        layer_pick,
        stored_qkv.astype(jnp.float32),
        precision=lax.Precision.HIGHEST,
        preferred_element_type=jnp.float32,
    )
    picked_gate = jnp.dot(
        layer_pick,
        stored_gate_up.astype(jnp.float32),
        precision=lax.Precision.HIGHEST,
        preferred_element_type=jnp.float32,
    )
    own_heads = lax.dynamic_slice_in_dim(head_slot, owner * slots, slots, 0)
    picked_qkv = picked_qkv[:, own_heads]
    picked_gate = (
        picked_gate.reshape(layers, 2, owners, blocks)
        .transpose(0, 2, 1, 3)
        .reshape(layers, owners * 2 * blocks)
    )
    picked_gate = lax.dynamic_slice_in_dim(picked_gate, owner * 2 * blocks, 2 * blocks, 1)
    qkv_mismatch = head_sum - picked_qkv * stored_unit
    gate_up_mismatch = block_sum - picked_gate * stored_unit
    return (served_qkv, served_gate, qkv_mismatch, gate_up_mismatch)


def solution(mesh):
    placed = (P(None, ("grp", "dev"), None), P(None, ("grp", "dev"), None), P(), P(), P(), P())
    return jax.shard_map(
        body,
        mesh=mesh,
        in_specs=placed,
        out_specs=(P(None, "grp", "dev"), P(None, "grp", "dev"), P(None, "dev"), P(None, "dev")),
        check_vma=False,
    )
```

profile of v0, /device:TPU:40, one launch (start us, length us, event | category | flops | bytes accessed | tf_op | source)
XLA Modules:
  0.0 289.1 jit_solution(16227011751404007670)
XLA Ops:
  0.6 0.0 copy-start
  0.7 0.8 compare_select_fusion.1
  1.4 0.7 compare_select_fusion
  2.1 4.0 %gather_fusion = bf16[64,2,36,128]{3,1,2,0:T(2,128)(2,1)S(1)} fusion(bf16[2,36,64,128]{3,0,2,1:T(2,128)(2,1)S(1)} %bitcast.22, s32[1024]{0:T(1024)S(1)} %get-tuple-element.35), kind=kCustom, calls=%fused_computation | custom fusion | bytes 2359552 | tf_op jit(solution)/shard_map/gather | solution.py:86
  6.2 0.3 copy.68
  6.5 0.4 reshape_reshape.12
  7.0 1.1 copy.69
  8.1 7.5 %all-to-all-start = ((bf16[32,2,16,1,1,256]{5,2,1,4,3,0:T(8,128)(2,1)}), bf16[32,2,16,1,1,256]{5,2,1,4,3,0:T(8,128)(2,1)S(1)}, u32[]{:S(2)}, u32[]{:S(2)}) async-start(bf16[32,2,16,1,1,256]{5,2,1,4,3,0:T(8,128)(2,1)} %copy.69), calls=%async_computation | async-start | bytes 1048576 | tf_op jit(solution)/shard_map/all_to_all | solution.py:41
  15.7 1.5 copy.70
  17.2 8.5 %all-to-all-done = bf16[32,2,16,1,1,256]{5,2,1,4,3,0:T(8,128)(2,1)S(1)} async-done(((bf16[32,2,16,1,1,256]{5,2,1,4,3,0:T(8,128)(2,1)}), bf16[32,2,16,1,1,256]{5,2,1,4,3,0:T(8,128)(2,1)S(1)}, u32[]{:S(2)}, u32[]{:S(2)}) %all-to-all-start) | async-done | bytes 524320 | tf_op jit(solution)/shard_map/all_to_all | solution.py:41
  25.6 5.2 %all-to-all-start.1 = ((bf16[32,2,20,1,1,256]{5,1,4,3,2,0:T(2,128)(2,1)}), bf16[32,2,20,1,1,256]{5,1,4,3,2,0:T(2,128)(2,1)S(1)}, u32[]{:S(2)}, u32[]{:S(2)}) async-start(bf16[32,2,20,1,1,256]{5,1,4,3,2,0:T(2,128)(2,1)} %copy.70), calls=%async_computation.1 | async-start | bytes 1310720 | tf_op jit(solution)/shard_map/all_to_all | solution.py:41
  30.8 24.3 %reshape_reshape.14 = bf16[2,36,2,32,1,1152]{5,3,2,0,1,4:T(8,128)(2,1)} reshape(bf16[2,36,73728]{2,0,1:T(2,128)(2,1)} %param.7) | data formatting | bytes 21233664 | tf_op jit(solution)/shard_map/reshape;reshape | solution.py:18
  55.2 5.1 %split.18 = bf16[32,2,16,2,1,1152]{5,0,3,1,2,4:T(8,128)(2,1)} slice(bf16[32,2,36,2,1,1152]{5,0,3,1,2,4:T(8,128)(2,1)} %bitcast.23), slice={[0:32], [0:2], [0:16], [0:2], [0:1], [0:1152]} | slice | bytes 9437184 | tf_op jit(solution)/shard_map/split | solution.py:39
  60.2 9.5 %copy.72 = bf16[32,2,16,2,1,1152]{5,3,2,1,4,0:T(2,128)(2,1)} copy(bf16[32,2,16,2,1,1152]{5,0,3,1,2,4:T(8,128)(2,1)} %split.18) | data formatting | bytes 9437184 | tf_op jit(solution)/shard_map/split | solution.py:39
  69.7 0.0 all-to-all-done.1
  69.7 7.4 %all-to-all-start.2 = ((bf16[32,2,16,2,1,1152]{5,3,2,1,4,0:T(2,128)(2,1)}), bf16[32,2,16,2,1,1152]{5,3,2,1,4,0:T(2,128)(2,1)}, u32[]{:S(2)}, u32[]{:S(2)}) async-start(bf16[32,2,16,2,1,1152]{5,3,2,1,4,0:T(2,128)(2,1)} %copy.72), calls=%async_computation.2 | async-start | bytes 9437184 | tf_op jit(solution)/shard_map/all_to_all | solution.py:41
  77.1 3.4 %split.19 = bf16[32,2,20,2,1,1152]{5,0,3,1,2,4:T(8,128)(2,1)S(1)} slice(bf16[32,2,36,2,1,1152]{5,0,3,1,2,4:T(8,128)(2,1)} %bitcast.24), slice={[0:32], [0:2], [16:36], [0:2], [0:1], [0:1152]} | slice | bytes 11796480 | tf_op jit(solution)/shard_map/split | solution.py:39
  80.5 7.4 %copy.73 = bf16[32,2,20,2,1,1152]{5,3,2,1,4,0:T(2,128)(2,1)} copy(bf16[32,2,20,2,1,1152]{5,0,3,1,2,4:T(8,128)(2,1)S(1)} %split.19) | data formatting | bytes 11796480 | tf_op jit(solution)/shard_map/split | solution.py:39
  87.9 51.0 %all-to-all-done.2 = bf16[32,2,16,2,1,1152]{5,3,2,1,4,0:T(2,128)(2,1)} async-done(((bf16[32,2,16,2,1,1152]{5,3,2,1,4,0:T(2,128)(2,1)}), bf16[32,2,16,2,1,1152]{5,3,2,1,4,0:T(2,128)(2,1)}, u32[]{:S(2)}, u32[]{:S(2)}) %all-to-all-start.2) | async-done | bytes 4718624 | tf_op jit(solution)/shard_map/all_to_all | solution.py:41
  138.9 4.7 %all-to-all-start.3 = ((bf16[32,2,20,2,1,1152]{5,3,2,1,4,0:T(2,128)(2,1)}), bf16[32,2,20,2,1,1152]{5,3,2,1,4,0:T(2,128)(2,1)}, u32[]{:S(2)}, u32[]{:S(2)}) async-start(bf16[32,2,20,2,1,1152]{5,3,2,1,4,0:T(2,128)(2,1)} %copy.73), calls=%async_computation.3 | async-start | bytes 11796480 | tf_op jit(solution)/shard_map/all_to_all | solution.py:41
  143.7 0.2 fusion
  143.9 0.1 reshape.55
  144.0 0.1 copy.78
  144.1 0.2 fusion.2
  144.3 0.4 copy_dynamic-update-slice_fusion
  144.7 0.5 constant_dynamic-update-slice_fusion
  145.2 1.2 convert_reduce_fusion.1
  146.5 0.1 reduce_sum.36
  146.6 0.1 reshape.51
  146.7 77.8 %all-to-all-done.3 = bf16[32,2,20,2,1,1152]{5,3,2,1,4,0:T(2,128)(2,1)} async-done(((bf16[32,2,20,2,1,1152]{5,3,2,1,4,0:T(2,128)(2,1)}), bf16[32,2,20,2,1,1152]{5,3,2,1,4,0:T(2,128)(2,1)}, u32[]{:S(2)}, u32[]{:S(2)}) %all-to-all-start.3) | async-done | bytes 5898272 | tf_op jit(solution)/shard_map/all_to_all | solution.py:41
  224.5 21.4 %convert_reduce_fusion = (f32[2,2,1152]{2,1,0:T(2,128)S(1)}, bf16[2,32,36,2,1,1152]{5,3,2,0,4,1:T(2,128)(2,1)}) fusion(bf16[32,2,20,2,1,1152]{5,3,2,1,4,0:T(2,128)(2,1)} %all-to-all-done.3, bf16[32,2,16,2,1,1152]{5,3,2,1,4,0:T(2,128)(2,1)} %all-to-all-done.2), kind=kLoop, calls=%fused_computation.2 | loop fusion | flops 15920640 | bytes 21252096 | tf_op jit(solution)/shard_map/reduce_sum | solution.py:72
  245.9 0.1 reduce_sum.46
  246.0 0.1 reshape.52
  246.1 0.1 pad_maximum_fusion
  246.2 0.5 broadcast_in_dim.12
  246.7 5.4 %all-to-all-start.4 = ((f32[4,1,40]{2,1,0:T(1,128)}), f32[4,1,40]{2,1,0:T(1,128)S(1)}, u32[]{:S(2)}, u32[]{:S(2)}) async-start(f32[4,1,40]{2,1,0:T(1,128)} %broadcast_in_dim.12), calls=%async_computation.4 | async-start | bytes 4096 | tf_op jit(solution)/shard_map/all_to_all | solution.py:47
  252.1 0.1 reshape.56
  252.3 0.6 gather_fusion.1
  252.8 1.2 copy.79
  254.0 10.2 %copy.74 = bf16[2,32,36,2,1,1152]{5,3,2,1,0,4:T(2,128)(2,1)} copy(bf16[2,32,36,2,1,1152]{5,3,2,0,4,1:T(2,128)(2,1)} %get-tuple-element.33) | data formatting | bytes 21233664 | tf_op jit(solution)/shard_map/transpose | solution.py:32
  264.2 23.2 %reshape_reshape.15 = bf16[2,1152,2304]{2,1,0:T(8,128)(2,1)} reshape(bf16[2,32,36,2,1,1152]{5,3,2,1,0,4:T(2,128)(2,1)} %copy.74) | data formatting | bytes 21233664 | tf_op jit(solution)/shard_map/reshape;reshape | solution.py:68
  287.4 0.0 all-to-all-done.4
  287.4 0.1 slice.15
  287.5 0.1 reshape.54
  287.6 0.1 reshape.53
  287.7 0.1 copy.77
  287.8 0.7 copy.80
  288.4 0.6 multiply_subtract_fusion
  (16 shorter events, 0.2 us)
Async XLA Ops:
  0.6 1.5 copy-start
  8.1 17.6 %all-to-all-start = ((bf16[32,2,16,1,1,256]{5,2,1,4,3,0:T(8,128)(2,1)}), bf16[32,2,16,1,1,256]{5,2,1,4,3,0:T(8,128)(2,1)S(1)}, u32[]{:S(2)}, u32[]{:S(2)}) async-start(bf16[32,2,16,1,1,256]{5,2,1,4,3,0:T(8,128)(2,1)} %copy.69), calls=%async_computation | async-start | bytes 1048576 | tf_op jit(solution)/shard_map/all_to_all | solution.py:41
  25.6 44.1 %all-to-all-start.1 = ((bf16[32,2,20,1,1,256]{5,1,4,3,2,0:T(2,128)(2,1)}), bf16[32,2,20,1,1,256]{5,1,4,3,2,0:T(2,128)(2,1)S(1)}, u32[]{:S(2)}, u32[]{:S(2)}) async-start(bf16[32,2,20,1,1,256]{5,1,4,3,2,0:T(2,128)(2,1)} %copy.70), calls=%async_computation.1 | async-start | bytes 1310720 | tf_op jit(solution)/shard_map/all_to_all | solution.py:41
  69.7 69.2 %all-to-all-start.2 = ((bf16[32,2,16,2,1,1152]{5,3,2,1,4,0:T(2,128)(2,1)}), bf16[32,2,16,2,1,1152]{5,3,2,1,4,0:T(2,128)(2,1)}, u32[]{:S(2)}, u32[]{:S(2)}) async-start(bf16[32,2,16,2,1,1152]{5,3,2,1,4,0:T(2,128)(2,1)} %copy.72), calls=%async_computation.2 | async-start | bytes 9437184 | tf_op jit(solution)/shard_map/all_to_all | solution.py:41
  87.9 55.7 %copy-start.2 = (s32[46,576]{1,0:T(8,128)S(1)}, s32[46,576]{1,0:T(8,128)}, u32[]{:S(2)}) copy-start(s32[46,576]{1,0:T(8,128)} %param.11) | copy-start | bytes 317956
  87.9 55.7 %copy-start.3 = (s32[2]{0:T(128)S(1)}, s32[2]{0:T(128)}, u32[]{:S(2)}) copy-start(s32[2]{0:T(128)} %param.9) | copy-start | bytes 28
  87.9 56.2 %copy-start.4 = (s32[46,64]{1,0:T(8,128)S(1)}, s32[46,64]{1,0:T(8,128)}, u32[]{:S(2)}) copy-start(s32[46,64]{1,0:T(8,128)} %param.10) | copy-start | bytes 35332
  138.9 85.5 %all-to-all-start.3 = ((bf16[32,2,20,2,1,1152]{5,3,2,1,4,0:T(2,128)(2,1)}), bf16[32,2,20,2,1,1152]{5,3,2,1,4,0:T(2,128)(2,1)}, u32[]{:S(2)}, u32[]{:S(2)}) async-start(bf16[32,2,20,2,1,1152]{5,3,2,1,4,0:T(2,128)(2,1)} %copy.73), calls=%async_computation.3 | async-start | bytes 11796480 | tf_op jit(solution)/shard_map/all_to_all | solution.py:41
  246.7 40.7 %all-to-all-start.4 = ((f32[4,1,40]{2,1,0:T(1,128)}), f32[4,1,40]{2,1,0:T(1,128)S(1)}, u32[]{:S(2)}, u32[]{:S(2)}) async-start(f32[4,1,40]{2,1,0:T(1,128)} %broadcast_in_dim.12), calls=%async_computation.4 | async-start | bytes 4096 | tf_op jit(solution)/shard_map/all_to_all | solution.py:47
  264.2 24.8 %copy-start.1 = (bf16[2,36,8192]{2,0,1:T(2,128)(2,1)S(1)}, bf16[2,36,8192]{2,0,1:T(2,128)(2,1)}, u32[]{:S(2)}) copy-start(bf16[2,36,8192]{2,0,1:T(2,128)(2,1)} %param.6) | copy-start | bytes 3538948
where the time goes:
time: 291 us; the launch traced here: 289 us
  waiting for transfers between devices  137 us (47%)
  local copies, waits for them, and re-layouts  95.2 us (33%)
  starting transfers between devices  30.3 us (10%)
  other arithmetic  25.1 us (9%)
    all_to_all x4, waiting for transfers between devices, several_exchanges(): lax.all_to_all(piece, axis, split_axis=0, concat_axis=0, tiled=True)  137 us
    split x8, local copies, waits for them, and re-layouts, several_exchanges(): jnp.split(blocks, piece_ends(blocks.shape[split_at], pieces), axis=split_at)  28 us
    all_to_all x4, starting transfers between devices, several_exchanges(): lax.all_to_all(piece, axis, split_axis=0, concat_axis=0, tiled=True)  24.8 us
    another operation x2, local copies, waits for them, and re-layouts, cut_along(): x.reshape(*dims[:dim], length, dims[dim] // length, *dims[dim + 1:])  24.8 us
    another operation x1, local copies, waits for them, and re-layouts, finish(): served_gate = gate_piece.reshape(count, height, 2 * gate_piece.shape[4])  23.2 us
    reduce_sum x2, other arithmetic, finish(): jnp.sum(served_gate.astype(jnp.float32).reshape(count, height, -1, BLK),...  21.5 us
    transpose x1, local copies, waits for them, and re-layouts, in_order(): return jnp.moveaxis(blocks, 0, dim).reshape(dims)  10.2 us
  transfers between devices with their start and end apart: 5, of which 3 were waited for; matrix products, arithmetic and copies ran while one was open for 31% of the time, Pallas kernels for 0%

commit v1 on v0

v1 whole, which is shorter than its diff:
```python
import functools

import jax
import jax.numpy as jnp
from jax import lax
from jax.experimental import pallas as pl
from jax.experimental.pallas import tpu as pltpu
from jax.sharding import PartitionSpec as P

HEAD_DIM = 128
FF = 36864
STORED = 46
BLK = 128
NHEAD = 64
LAYERS = 2
ROWS = 36
N_DEV = 32
N_GRP = 4
WIDTH = FF // N_DEV
BLOCKS = WIDTH // BLK
SLOTS = NHEAD // N_DEV
QW = SLOTS * HEAD_DIM

stored_unit = 1.0 / 1024.0
MESH = pl.DeviceIdType.MESH

FAR_X = ((2, 1, 0, 1), (0, 1, 0, 1), (2, -1, 0, 1), (0, -1, 0, 1))
FAR_Y = ((1, 2, 1, 0), (-1, 0, 1, 0), (-1, 2, 1, 0), (1, 0, 1, 0))
DIAGONAL = ((1, 1, 1, 0), (-1, -1, 1, 0), (1, -1, 1, 0), (-1, 1, 1, 0))
OPPOSITE = ((2, 0, 0, 0), (0, 2, 0, 0), (2, 2, 0, 0))
ROUNDS = (FAR_X, FAR_Y, DIAGONAL, OPPOSITE)


def owner_at(me, offset, flip):
    dx, dy, mirror_x, mirror_y = offset
    x, y, core = me // 8, (me // 2) % 4, me % 2
    sign = 1 - 2 * core
    x = (x + (dx * sign if mirror_x else dx) + 4) % 4
    y = (y + (dy * sign if mirror_y else dy) + 4) % 4
    return (x * 4 + y) * 2 + (core + flip) % 2


def kernel(
    gate, qkv, slot_ref, layer_ref, stored_q, stored_g,
    gate_out, qkv_out, mismatch,
    qkv_in, qkv_send, rows_in, sum_send, sum_recv, part_send, part_recv, table_q, table_g,
    gate_sem, qkv_sem, sum_sem, part_sem, own_sem, load_sem, table_sem,
):
    me = lax.axis_index("dev")
    grp = lax.axis_index("grp")

    load_tq = pltpu.make_async_copy(stored_q, table_q, table_sem.at[1])
    load_tg = pltpu.make_async_copy(stored_g, table_g, table_sem.at[2])

    def load_head(head, _):
        column = pl.ds(pl.multiple_of(head * HEAD_DIM, HEAD_DIM), HEAD_DIM)
        pltpu.make_async_copy(qkv.at[:, :, column], qkv_in.at[head], table_sem.at[0]).start()
        return 0

    lax.fori_loop(0, NHEAD, load_head, 0)
    load_tq.start()
    load_tg.start()

    barrier = pltpu.get_barrier_semaphore()

    def greet(k, _):
        pl.semaphore_signal(barrier, inc=1, device_id={"dev": (me + k) % N_DEV}, device_id_type=MESH)
        return 0

    lax.fori_loop(1, N_DEV, greet, 0)
    for k in range(1, N_GRP):
        pl.semaphore_signal(barrier, inc=1, device_id={"grp": (grp + k) % N_GRP}, device_id_type=MESH)
    pl.semaphore_wait(barrier, N_DEV + N_GRP - 2)

    own_rows = pl.ds(me * ROWS, ROWS)

    def send_gate(owner, p):
        pltpu.make_async_remote_copy(
            src_ref=gate.at[:, :, pl.ds(pl.multiple_of(p * FF + owner * WIDTH, BLK), WIDTH)],
            dst_ref=gate_out.at[own_rows, :, pl.ds(pl.multiple_of(p * WIDTH, BLK), WIDTH)],
            send_sem=gate_sem.at[0],
            recv_sem=gate_sem.at[1],
            device_id={"dev": owner},
            device_id_type=MESH,
        ).start()

    def send_qkv(owner):
        pltpu.make_async_remote_copy(
            src_ref=qkv_send.at[owner],
            dst_ref=qkv_out.at[own_rows],
            send_sem=qkv_sem.at[0],
            recv_sem=qkv_sem.at[1],
            device_id={"dev": owner},
            device_id_type=MESH,
        ).start()

    def gate_round(offsets):
        def step(i, _):
            for offset in offsets:
                send_gate(owner_at(me, offset, i % 2), i // 2)
            return 0

        lax.fori_loop(0, 4, step, 0)

    partner = owner_at(me, (0, 0, 0, 0), 1)
    own_copies = []
    for p in range(2):
        send_gate(partner, p)
        own_copies.append(
            pltpu.make_async_copy(
                gate.at[:, :, pl.ds(pl.multiple_of(p * FF + me * WIDTH, BLK), WIDTH)],
                gate_out.at[own_rows, :, pl.ds(p * WIDTH, WIDTH)],
                own_sem.at[p],
            )
        )
    gate_round(ROUNDS[0])
    gate_round(ROUNDS[1])
    for copy in own_copies:
        copy.start()

    pltpu.make_async_copy(qkv_in, qkv_in, table_sem.at[0]).wait()

    def place(slot, _):
        part = qkv_in[slot_ref[slot]]
        column = pl.ds(pl.multiple_of((slot % SLOTS) * HEAD_DIM, HEAD_DIM), HEAD_DIM)
        qkv_send[slot // SLOTS, :, :, column] = part
        return 0

    lax.fori_loop(0, NHEAD, place, 0)

    def load(owner, slot):
        return [
            pltpu.make_async_copy(
                gate.at[:, :, pl.ds(pl.multiple_of(p * FF + owner * WIDTH, BLK), WIDTH)],
                rows_in.at[slot, p],
                load_sem.at[slot, p],
            )
            for p in range(2)
        ]

    lane = lax.broadcasted_iota(jnp.int32, (LAYERS, 128), 1)

    def block_total(values, at, total):
        rows = jnp.sum(values.astype(jnp.float32), axis=0)
        return jnp.where(lane == at, jnp.sum(rows, axis=1, keepdims=True), total)

    for copy in load(0, 0):
        copy.start()

    def add_up(owner, _):
        slot = owner % 2

        @pl.when(owner + 1 < N_DEV)
        def _():
            for copy in load(owner + 1, 1 - slot):
                copy.start()

        for copy in load(owner, slot):
            copy.wait()
        total = jnp.zeros((LAYERS, 128), jnp.float32)
        for p in range(2):
            for b in range(BLOCKS):
                total = block_total(rows_in[slot, p, :, :, b * BLK : (b + 1) * BLK], p * BLOCKS + b, total)
        for s in range(SLOTS):
            total = block_total(
                qkv_send[owner, :, :, s * HEAD_DIM : (s + 1) * HEAD_DIM], 2 * BLOCKS + s, total
            )
        sum_send[owner] = total
        return 0

    lax.fori_loop(0, N_DEV, add_up, 0)

    own_copies.append(pltpu.make_async_copy(qkv_send.at[me], qkv_out.at[own_rows], own_sem.at[2]))
    own_copies[2].start()

    def send_qkv_round(offsets, flip):
        for offset in offsets:
            send_qkv(owner_at(me, offset, flip))

    def small_sends(i, _):
        owner = (me + i) % N_DEV
        pltpu.make_async_remote_copy(
            src_ref=sum_send.at[owner],
            dst_ref=sum_recv.at[me],
            send_sem=sum_sem.at[0],
            recv_sem=sum_sem.at[1],
            device_id={"dev": owner},
            device_id_type=MESH,
        ).start()
        return 0

    lax.fori_loop(1, N_DEV, small_sends, 0)
    send_qkv(partner)

    def qkv_sends(flip, _):
        for offsets in ROUNDS:
            send_qkv_round(offsets, flip)
        return 0

    lax.fori_loop(0, 2, qkv_sends, 0)
    gate_round(ROUNDS[2])
    gate_round(ROUNDS[3])

    sum_recv[me] = sum_send[me]

    load_tq.wait()
    load_tg.wait()
    row_of = lax.broadcasted_iota(jnp.int32, (8, STORED), 0)
    layer_of = lax.broadcasted_iota(jnp.int32, (8, STORED), 1)
    wanted = jnp.where(row_of == 0, layer_ref[0], layer_ref[1])
    layer_pick = jnp.where((layer_of == wanted) & (row_of < LAYERS), 1.0, 0.0).astype(jnp.float32)

    def picked(table, columns):
        dot = functools.partial(
            jnp.dot, precision=lax.Precision.HIGHEST, preferred_element_type=jnp.float32
        )
        return dot(dot(layer_pick, table.astype(jnp.float32)), columns)

    blocks = 2 * FF // BLK
    block_of = lax.broadcasted_iota(jnp.int32, (blocks, 128), 0)
    to = lax.broadcasted_iota(jnp.int32, (blocks, 128), 1)
    source = me * BLOCKS + jnp.where(to < BLOCKS, to, FF // BLK + to - BLOCKS)
    pick_g = jnp.where((block_of == source) & (to < 2 * BLOCKS), 1.0, 0.0).astype(jnp.float32)
    head_of = lax.broadcasted_iota(jnp.int32, (NHEAD, 128), 0)
    to = lax.broadcasted_iota(jnp.int32, (NHEAD, 128), 1)
    pick_q = jnp.zeros((NHEAD, 128), jnp.float32)
    for s in range(SLOTS):
        hit = (head_of == slot_ref[me * SLOTS + s]) & (to == 2 * BLOCKS + s)
        pick_q = jnp.where(hit, 1.0, pick_q)
    expected = (picked(table_g[...], pick_g) + picked(table_q[...], pick_q)) * stored_unit

    others = pl.ds(0, N_DEV - 1)
    pltpu.make_async_copy(sum_recv.at[others], sum_recv.at[others], sum_sem.at[1]).wait()
    part_send[...] = jnp.sum(sum_recv[...], axis=0)
    part_recv[0] = part_send[...]
    for k in range(1, N_GRP):
        pltpu.make_async_remote_copy(
            src_ref=part_send,
            dst_ref=part_recv.at[k],
            send_sem=part_sem.at[0],
            recv_sem=part_sem.at[1],
            device_id={"grp": (grp + k) % N_GRP},
            device_id_type=MESH,
        ).start()
    parts = pl.ds(1, N_GRP - 1)
    pltpu.make_async_copy(part_recv.at[parts], part_recv.at[parts], part_sem.at[1]).wait()
    mismatch[...] = jnp.sum(part_recv[...], axis=0) - expected[:LAYERS]

    pltpu.make_async_copy(part_recv.at[parts], part_recv.at[parts], part_sem.at[0]).wait()
    pltpu.make_async_copy(sum_recv.at[others], sum_recv.at[others], sum_sem.at[0]).wait()
    for copy in own_copies:
        copy.wait()
    moved = pl.ds(0, (N_DEV - 1) * ROWS)
    for at in range(2):
        pltpu.make_async_copy(qkv_out.at[moved], qkv_out.at[moved], qkv_sem.at[at]).wait()
        pltpu.make_async_copy(gate_out.at[moved], gate_out.at[moved], gate_sem.at[at]).wait()


def body(qkv_weight, gate_up_weight, head_slot, layer_ids, stored_qkv, stored_gate_up):
    anywhere = pl.BlockSpec(memory_space=pl.ANY)
    scalars = pl.BlockSpec(memory_space=pltpu.SMEM)
    in_vmem = pl.BlockSpec(memory_space=pltpu.VMEM)
    total_rows = N_DEV * ROWS
    gate, qkv, mismatch = pl.pallas_call(
        kernel,
        out_shape=(
            jax.ShapeDtypeStruct((total_rows, LAYERS, 2 * WIDTH), jnp.bfloat16),
            jax.ShapeDtypeStruct((total_rows, LAYERS, QW), jnp.bfloat16),
            jax.ShapeDtypeStruct((LAYERS, 128), jnp.float32),
        ),
        in_specs=[anywhere, anywhere, scalars, scalars, anywhere, anywhere],
        out_specs=(anywhere, anywhere, in_vmem),
        scratch_shapes=[
            pltpu.VMEM((NHEAD, ROWS, LAYERS, HEAD_DIM), jnp.bfloat16),
            pltpu.VMEM((N_DEV, ROWS, LAYERS, QW), jnp.bfloat16),
            pltpu.VMEM((2, 2, ROWS, LAYERS, WIDTH), jnp.bfloat16),
            pltpu.VMEM((N_DEV, LAYERS, 128), jnp.float32),
            pltpu.VMEM((N_DEV, LAYERS, 128), jnp.float32),
            pltpu.VMEM((LAYERS, 128), jnp.float32),
            pltpu.VMEM((N_GRP, LAYERS, 128), jnp.float32),
            pltpu.VMEM((STORED, NHEAD), jnp.int32),
            pltpu.VMEM((STORED, 2 * FF // BLK), jnp.int32),
            pltpu.SemaphoreType.DMA((2,)),
            pltpu.SemaphoreType.DMA((2,)),
            pltpu.SemaphoreType.DMA((2,)),
            pltpu.SemaphoreType.DMA((2,)),
            pltpu.SemaphoreType.DMA((3,)),
            pltpu.SemaphoreType.DMA((2, 2)),
            pltpu.SemaphoreType.DMA((3,)),
        ],
        compiler_params=pltpu.CompilerParams(collective_id=0, has_side_effects=True),
        name="exchange",
    )(
        gate_up_weight.transpose(1, 0, 2),
        qkv_weight.transpose(1, 0, 2),
        head_slot,
        layer_ids,
        stored_qkv,
        stored_gate_up,
    )
    return (
        qkv.transpose(1, 0, 2),
        gate.transpose(1, 0, 2),
        mismatch[:, 2 * BLOCKS : 2 * BLOCKS + SLOTS],
        mismatch[:, : 2 * BLOCKS],
    )


def solution(mesh):
    placed = (P(None, ("grp", "dev"), None), P(None, ("grp", "dev"), None), P(), P(), P(), P())
    return jax.shard_map(
        body,
        mesh=mesh,
        in_specs=placed,
        out_specs=(P(None, "grp", "dev"), P(None, "grp", "dev"), P(None, "dev"), P(None, "dev")),
        check_vma=False,
    )
```

time: 291 us -> 165 us (0.57)
  Pallas kernels: 0 us -> 146 us
  waiting for transfers between devices: 137 us -> 0 us
  local copies, waits for them, and re-layouts: 95.2 us -> 14.8 us
  starting transfers between devices: 30.3 us -> 0 us
  other arithmetic: 25.1 us -> 0 us
    pallas_call x0 -> x1, Pallas kernels: none -> 146 us  [body(): pl.pallas_call(kernel, out_shape=(jax.ShapeDtypeStruct((total_rows, LAYER...]
    all_to_all x5 -> x0, waiting for transfers between devices: 137 us -> none  [the longest x4 137 us: several_exchanges(): lax.all_to_all(piece, axis, split_axis=0, concat_axis=0, tiled=True)]
    another operation x3 -> x0, local copies, waits for them, and re-layouts: 48 us -> none  [the longest x2 24.8 us: cut_along(): x.reshape(*dims[:dim], length, dims[dim] // length, *dims[dim + 1:])]
    all_to_all x5 -> x0, starting transfers between devices: 30.3 us -> none  [the longest x4 24.8 us: several_exchanges(): lax.all_to_all(piece, axis, split_axis=0, concat_axis=0, tiled=True)]
    split x8 -> x0, local copies, waits for them, and re-layouts: 28 us -> none  [several_exchanges(): jnp.split(blocks, piece_ends(blocks.shape[split_at], pieces), axis=split_at)]
    reduce_sum x5 -> x0, other arithmetic: 22.9 us -> none  [the longest x2 21.5 us: finish(): jnp.sum(served_gate.astype(jnp.float32).reshape(count, height, -1, BLK),...]
    unnamed x13 -> x5, local copies, waits for them, and re-layouts: 2.25 us -> 14.2 us
    transpose x2 -> x0, local copies, waits for them, and re-layouts: 10.3 us -> none  [the longest x1 10.2 us: in_order(): return jnp.moveaxis(blocks, 0, dim).reshape(dims)]
  transfers between devices with their start and end apart: 5 -> 0, of which waited for: 3 -> 0; matrix products, arithmetic and copies ran while one was open for 31% -> 0% of each run, Pallas kernels for 0% -> 0%
where the time goes in v1:
time: 165 us; the launch traced here: 162 us
  Pallas kernels  146 us (88%)
  local copies, waits for them, and re-layouts  14.8 us (9%)
    pallas_call x1, Pallas kernels, body(): pl.pallas_call(kernel, out_shape=(jax.ShapeDtypeStruct((total_rows, LAYER...  146 us
    unnamed x5, local copies, waits for them, and re-layouts  14.2 us

profile of v1, /device:TPU:40, one launch (start us, length us, event | category | flops | bytes accessed | tf_op | source)
XLA Modules:
  0.0 161.7 jit_solution(6105203478601174933)
XLA Ops:
  0.6 146.2 %exchange.1 = (bf16[1152,2,2304]{2,1,0:T(2,128)(2,1)}, bf16[1152,2,256]{2,1,0:T(2,128)(2,1)}, f32[2,128]{1,0:T(2,128)}) custom-call(bf16[36,2,73728]{2,1,0:T(2,128)(2,1)} %bitcast.5, bf16[36,2,8192]{2,1,0:T(2,128)(2,1)} %bitcast.7, s32[64]{0:T(128)} %slot_ref.1, s32[2]{0:T(128)} %layer_ref.1, s32[46,64]{1,0:T(8,128)} %stored_q.1, s32[46,576]{1,0:T(8,128)} %stored_g.1), custom_call_target="tpu_custom_call" | custom-call | tf_op jit(solution)/shard_map/exchange/pallas_call | solution.py:264
  146.9 2.4 %copy.10 = bf16[2,1152,256]{2,1,0:T(8,128)(2,1)} copy(bf16[2,1152,256]{2,0,1:T(2,128)(2,1)} %bitcast.8) | data formatting | bytes 2359296
  149.3 0.0 copy-start
  149.3 11.2 %copy.11 = bf16[2,1152,2304]{2,1,0:T(8,128)(2,1)} copy(bf16[2,1152,2304]{2,0,1:T(2,128)(2,1)} %bitcast.6) | data formatting | bytes 21233664
  160.5 0.0 copy-done
  160.5 0.6 slice.6
  161.1 0.6 copy.13
Async XLA Ops:
  149.3 11.2 %copy-start = (f32[2,128]{1,0:T(2,128)S(1)}, f32[2,128]{1,0:T(2,128)}, u32[]{:S(2)}) copy-start(f32[2,128]{1,0:T(2,128)} %get-tuple-element.9) | copy-start | bytes 3076

commit v2 on v1

--- a/solution.py
+++ b/solution.py
@@ -43,8 +43,9 @@
 def kernel(
     gate, qkv, slot_ref, layer_ref, stored_q, stored_g,
     gate_out, qkv_out, mismatch,
-    qkv_in, qkv_send, rows_in, sum_send, sum_recv, part_send, part_recv, table_q, table_g,
-    gate_sem, qkv_sem, sum_sem, part_sem, own_sem, load_sem, table_sem,
+    gate_land, qkv_land,
+    qkv_in, qkv_send, rows_in, sum_send, sum_recv, part_send, part_recv, part_total, part_land,
+    table_q, table_g, gate_sem, gate_recv, qkv_sem, qkv_recv, sum_sem, part_sem, load_sem, table_sem,
 ):
     me = lax.axis_index("dev")
     grp = lax.axis_index("grp")
@@ -68,18 +69,22 @@
         return 0
 
     lax.fori_loop(1, N_DEV, greet, 0)
-    for k in range(1, N_GRP):
-        pl.semaphore_signal(barrier, inc=1, device_id={"grp": (grp + k) % N_GRP}, device_id_type=MESH)
-    pl.semaphore_wait(barrier, N_DEV + N_GRP - 2)
+
+    def greet_later(k, _):
+        pl.semaphore_signal(barrier, inc=1, device_id={"grp": k}, device_id_type=MESH)
+        return 0
+
+    lax.fori_loop(grp + 1, N_GRP, greet_later, 0)
+    pl.semaphore_wait(barrier, N_DEV - 1 + grp)
 
     own_rows = pl.ds(me * ROWS, ROWS)
 
     def send_gate(owner, p):
         pltpu.make_async_remote_copy(
             src_ref=gate.at[:, :, pl.ds(pl.multiple_of(p * FF + owner * WIDTH, BLK), WIDTH)],
-            dst_ref=gate_out.at[own_rows, :, pl.ds(pl.multiple_of(p * WIDTH, BLK), WIDTH)],
-            send_sem=gate_sem.at[0],
-            recv_sem=gate_sem.at[1],
+            dst_ref=gate_land.at[own_rows, :, pl.ds(pl.multiple_of(p * WIDTH, BLK), WIDTH)],
+            send_sem=gate_sem,
+            recv_sem=gate_recv.at[me],
             device_id={"dev": owner},
             device_id_type=MESH,
         ).start()
@@ -87,9 +92,9 @@
     def send_qkv(owner):
         pltpu.make_async_remote_copy(
             src_ref=qkv_send.at[owner],
-            dst_ref=qkv_out.at[own_rows],
-            send_sem=qkv_sem.at[0],
-            recv_sem=qkv_sem.at[1],
+            dst_ref=qkv_land.at[own_rows],
+            send_sem=qkv_sem,
+            recv_sem=qkv_recv.at[me],
             device_id={"dev": owner},
             device_id_type=MESH,
         ).start()
@@ -103,20 +108,16 @@
         lax.fori_loop(0, 4, step, 0)
 
     partner = owner_at(me, (0, 0, 0, 0), 1)
-    own_copies = []
     for p in range(2):
         send_gate(partner, p)
-        own_copies.append(
-            pltpu.make_async_copy(
-                gate.at[:, :, pl.ds(pl.multiple_of(p * FF + me * WIDTH, BLK), WIDTH)],
-                gate_out.at[own_rows, :, pl.ds(p * WIDTH, WIDTH)],
-                own_sem.at[p],
-            )
-        )
     gate_round(ROUNDS[0])
     gate_round(ROUNDS[1])
-    for copy in own_copies:
-        copy.start()
+    for p in range(2):
+        pltpu.make_async_copy(
+            gate.at[:, :, pl.ds(pl.multiple_of(p * FF + me * WIDTH, BLK), WIDTH)],
+            gate_land.at[own_rows, :, pl.ds(p * WIDTH, WIDTH)],
+            gate_recv.at[me],
+        ).start()
 
     pltpu.make_async_copy(qkv_in, qkv_in, table_sem.at[0]).wait()
 
@@ -170,9 +171,6 @@
 
     lax.fori_loop(0, N_DEV, add_up, 0)
 
-    own_copies.append(pltpu.make_async_copy(qkv_send.at[me], qkv_out.at[own_rows], own_sem.at[2]))
-    own_copies[2].start()
-
     def send_qkv_round(offsets, flip):
         for offset in offsets:
             send_qkv(owner_at(me, offset, flip))
@@ -202,6 +200,7 @@
     gate_round(ROUNDS[3])
 
     sum_recv[me] = sum_send[me]
+    qkv_land[own_rows] = qkv_send[me]
 
     load_tq.wait()
     load_tg.wait()
@@ -229,31 +228,101 @@
         pick_q = jnp.where(hit, 1.0, pick_q)
     expected = (picked(table_g[...], pick_g) + picked(table_q[...], pick_q)) * stored_unit
 
+    def take_apart(land, out, chip, column):
+        start = pl.multiple_of(chip * 2 * ROWS, 8)
+        rows = land[pl.ds(start, 2 * ROWS), :, column].reshape(2 * ROWS // 8, 8, LAYERS, BLK)
+        rows = jnp.swapaxes(rows, 1, 2)
+        for i in range(2 * ROWS // 8):
+            for layer in range(LAYERS):
+                out[layer, pl.ds(pl.multiple_of(start + 8 * i, 8), 8), column] = rows[i, layer]
+
+    def settle(land, out, landed, width, offset, only=None):
+        x, y = me // 8, (me // 2) % 4
+        chip = (x + offset[0] + 4) % 4 * 4 + (y + offset[1] + 4) % 4
+        for core in range(2):
+            source = chip * 2 + core
+            block = land.at[pl.ds(source * ROWS, ROWS)]
+            wait = pltpu.make_async_copy(block, block, landed.at[source]).wait
+            if only is None:
+                wait()
+            else:
+                pl.when(source != me)(wait)
+
+        def step(i, _):
+            take_apart(land, out, chip, pl.ds(pl.multiple_of(i * BLK, BLK), BLK))
+            return 0
+
+        lax.fori_loop(0, width // BLK, step, 0)
+
+    def settle_gate(offsets):
+        for offset in offsets:
+            settle(gate_land, gate_out, gate_recv, 2 * WIDTH, offset)
+
+    here = ((0, 0),)
+    settle_gate(here)
+    settle_gate(ROUNDS[0])
+    settle_gate(ROUNDS[1])
+
     others = pl.ds(0, N_DEV - 1)
     pltpu.make_async_copy(sum_recv.at[others], sum_recv.at[others], sum_sem.at[1]).wait()
     part_send[...] = jnp.sum(sum_recv[...], axis=0)
-    part_recv[0] = part_send[...]
-    for k in range(1, N_GRP):
-        pltpu.make_async_remote_copy(
-            src_ref=part_send,
-            dst_ref=part_recv.at[k],
-            send_sem=part_sem.at[0],
-            recv_sem=part_sem.at[1],
-            device_id={"grp": (grp + k) % N_GRP},
+    to_first = pltpu.make_async_remote_copy(
+        src_ref=part_send,
+        dst_ref=part_recv.at[grp],
+        send_sem=part_sem.at[0],
+        recv_sem=part_sem.at[1],
+        device_id={"grp": 0},
+        device_id_type=MESH,
+    )
+
+    @pl.when(grp > 0)
+    def _():
+        to_first.start()
+
+    settle(qkv_land, qkv_out, qkv_recv, QW, here[0], only="others")
+    for offsets in ROUNDS:
+        for offset in offsets:
+            settle(qkv_land, qkv_out, qkv_recv, QW, offset)
+    parts = pl.ds(1, N_GRP - 1)
+    from_others = part_recv.at[parts]
+
+    def total_to(k):
+        return pltpu.make_async_remote_copy(
+            src_ref=part_total,
+            dst_ref=part_land,
+            send_sem=part_sem.at[2],
+            recv_sem=part_sem.at[3],
+            device_id={"grp": k},
             device_id_type=MESH,
-        ).start()
-    parts = pl.ds(1, N_GRP - 1)
-    pltpu.make_async_copy(part_recv.at[parts], part_recv.at[parts], part_sem.at[1]).wait()
-    mismatch[...] = jnp.sum(part_recv[...], axis=0) - expected[:LAYERS]
-
-    pltpu.make_async_copy(part_recv.at[parts], part_recv.at[parts], part_sem.at[0]).wait()
+        )
+
+    @pl.when(grp == 0)
+    def _():
+        part_recv[0] = part_send[...]
+        pltpu.make_async_copy(from_others, from_others, part_sem.at[1]).wait()
+        total = jnp.sum(part_recv[...], axis=0)
+        part_total[...] = total
+        mismatch[...] = total - expected[:LAYERS]
+        for k in range(1, N_GRP):
+            total_to(k).start()
+
+    settle_gate(ROUNDS[2])
+    settle_gate(ROUNDS[3])
+
+    @pl.when(grp > 0)
+    def _():
+        pltpu.make_async_copy(part_land, part_land, part_sem.at[3]).wait()
+        mismatch[...] = part_land[...] - expected[:LAYERS]
+        to_first.wait_send()
+
+    @pl.when(grp == 0)
+    def _():
+        pltpu.make_async_copy(from_others, from_others, part_sem.at[2]).wait()
+
     pltpu.make_async_copy(sum_recv.at[others], sum_recv.at[others], sum_sem.at[0]).wait()
-    for copy in own_copies:
-        copy.wait()
     moved = pl.ds(0, (N_DEV - 1) * ROWS)
-    for at in range(2):
-        pltpu.make_async_copy(qkv_out.at[moved], qkv_out.at[moved], qkv_sem.at[at]).wait()
-        pltpu.make_async_copy(gate_out.at[moved], gate_out.at[moved], gate_sem.at[at]).wait()
+    pltpu.make_async_copy(qkv_land.at[moved], qkv_land.at[moved], qkv_sem).wait()
+    pltpu.make_async_copy(gate_land.at[moved], gate_land.at[moved], gate_sem).wait()
 
 
 def body(qkv_weight, gate_up_weight, head_slot, layer_ids, stored_qkv, stored_gate_up):
@@ -264,13 +333,15 @@
     gate, qkv, mismatch = pl.pallas_call(
         kernel,
         out_shape=(
-            jax.ShapeDtypeStruct((total_rows, LAYERS, 2 * WIDTH), jnp.bfloat16),
-            jax.ShapeDtypeStruct((total_rows, LAYERS, QW), jnp.bfloat16),
-            jax.ShapeDtypeStruct((LAYERS, 128), jnp.float32),
+            pltpu.VMEM((LAYERS, total_rows, 2 * WIDTH), jnp.bfloat16),
+            pltpu.VMEM((LAYERS, total_rows, QW), jnp.bfloat16),
+            pltpu.VMEM((LAYERS, 128), jnp.float32),
         ),
         in_specs=[anywhere, anywhere, scalars, scalars, anywhere, anywhere],
-        out_specs=(anywhere, anywhere, in_vmem),
+        out_specs=(in_vmem, in_vmem, in_vmem),
         scratch_shapes=[
+            pltpu.VMEM((total_rows, LAYERS, 2 * WIDTH), jnp.bfloat16),
+            pltpu.VMEM((total_rows, LAYERS, QW), jnp.bfloat16),
             pltpu.VMEM((NHEAD, ROWS, LAYERS, HEAD_DIM), jnp.bfloat16),
             pltpu.VMEM((N_DEV, ROWS, LAYERS, QW), jnp.bfloat16),
             pltpu.VMEM((2, 2, ROWS, LAYERS, WIDTH), jnp.bfloat16),
@@ -278,17 +349,22 @@
             pltpu.VMEM((N_DEV, LAYERS, 128), jnp.float32),
             pltpu.VMEM((LAYERS, 128), jnp.float32),
             pltpu.VMEM((N_GRP, LAYERS, 128), jnp.float32),
+            pltpu.VMEM((LAYERS, 128), jnp.float32),
+            pltpu.VMEM((LAYERS, 128), jnp.float32),
             pltpu.VMEM((STORED, NHEAD), jnp.int32),
             pltpu.VMEM((STORED, 2 * FF // BLK), jnp.int32),
+            pltpu.SemaphoreType.DMA,
+            pltpu.SemaphoreType.DMA((N_DEV,)),
+            pltpu.SemaphoreType.DMA,
+            pltpu.SemaphoreType.DMA((N_DEV,)),
             pltpu.SemaphoreType.DMA((2,)),
-            pltpu.SemaphoreType.DMA((2,)),
-            pltpu.SemaphoreType.DMA((2,)),
-            pltpu.SemaphoreType.DMA((2,)),
-            pltpu.SemaphoreType.DMA((3,)),
+            pltpu.SemaphoreType.DMA((4,)),
             pltpu.SemaphoreType.DMA((2, 2)),
             pltpu.SemaphoreType.DMA((3,)),
         ],
-        compiler_params=pltpu.CompilerParams(collective_id=0, has_side_effects=True),
+        compiler_params=pltpu.CompilerParams(
+            collective_id=0, has_side_effects=True, vmem_limit_bytes=50 << 20
+        ),
         name="exchange",
     )(
         gate_up_weight.transpose(1, 0, 2),
@@ -299,8 +375,8 @@
         stored_gate_up,
     )
     return (
-        qkv.transpose(1, 0, 2),
-        gate.transpose(1, 0, 2),
+        qkv,
+        gate,
         mismatch[:, 2 * BLOCKS : 2 * BLOCKS + SLOTS],
         mismatch[:, : 2 * BLOCKS],
     )

time: 165 us -> 150 us (0.909)
  local copies, waits for them, and re-layouts: 14.8 us -> 6.34 us
  Pallas kernels: 146 us -> 140 us
    unnamed x5 -> x3, local copies, waits for them, and re-layouts: 14.2 us -> 5.71 us
    pallas_call x1, Pallas kernels: 146 us -> 140 us  [body(): pl.pallas_call(kernel, out_shape=(pltpu.VMEM((LAYERS, total_rows, 2 * WID...]
where the time goes in v2:
time: 150 us; the launch traced here: 147 us
  Pallas kernels  140 us (93%)
  local copies, waits for them, and re-layouts  6.34 us (4%)
    pallas_call x1, Pallas kernels, body(): pl.pallas_call(kernel, out_shape=(pltpu.VMEM((LAYERS, total_rows, 2 * WID...  140 us
    unnamed x3, local copies, waits for them, and re-layouts  5.71 us

profile of v2, /device:TPU:40, one launch (start us, length us, event | category | flops | bytes accessed | tf_op | source)
XLA Modules:
  0.0 147.5 jit_solution(9033420365193834666)
XLA Ops:
  0.6 140.5 %exchange.1 = (bf16[2,1152,2304]{2,1,0:T(8,128)(2,1)S(1)}, bf16[2,1152,256]{2,1,0:T(8,128)(2,1)S(1)}, f32[2,128]{1,0:T(2,128)S(1)}) custom-call(bf16[36,2,73728]{2,1,0:T(2,128)(2,1)} %bitcast.4, bf16[36,2,8192]{2,1,0:T(2,128)(2,1)} %bitcast.5, s32[64]{0:T(128)} %slot_ref.1, s32[2]{0:T(128)} %layer_ref.1, s32[46,64]{1,0:T(8,128)} %stored_q.1, s32[46,576]{1,0:T(8,128)} %stored_g.1), custom_call_target="tpu_custom_call" | custom-call | tf_op jit(solution)/shard_map/exchange/pallas_call | solution.py:333
  141.1 1.0 copy.13
  142.1 4.1 %copy.14 = bf16[2,1152,2304]{2,1,0:T(8,128)(2,1)} copy(bf16[2,1152,2304]{2,1,0:T(8,128)(2,1)S(1)} %get-tuple-element.11) | data formatting | bytes 21233664
  146.3 0.6 slice.6
  146.9 0.6 copy.15

commit v3 on v2

--- a/solution.py
+++ b/solution.py
@@ -20,6 +20,7 @@
 BLOCKS = WIDTH // BLK
 SLOTS = NHEAD // N_DEV
 QW = SLOTS * HEAD_DIM
+PIECES = 4
 
 stored_unit = 1.0 / 1024.0
 MESH = pl.DeviceIdType.MESH
@@ -28,7 +29,7 @@
 FAR_Y = ((1, 2, 1, 0), (-1, 0, 1, 0), (-1, 2, 1, 0), (1, 0, 1, 0))
 DIAGONAL = ((1, 1, 1, 0), (-1, -1, 1, 0), (1, -1, 1, 0), (-1, 1, 1, 0))
 OPPOSITE = ((2, 0, 0, 0), (0, 2, 0, 0), (2, 2, 0, 0))
-ROUNDS = (FAR_X, FAR_Y, DIAGONAL, OPPOSITE)
+ROUNDS = (FAR_X, OPPOSITE, FAR_Y, DIAGONAL)
 
 
 def owner_at(me, offset, flip):
@@ -41,26 +42,14 @@
 
 
 def kernel(
-    gate, qkv, slot_ref, layer_ref, stored_q, stored_g,
-    gate_out, qkv_out, mismatch,
+    gate, qkv, head_slot, layer_ids, stored_q, stored_g,
+    gate_out, qkv_out, qkv_mismatch, gate_mismatch,
     gate_land, qkv_land,
     qkv_in, qkv_send, rows_in, sum_send, sum_recv, part_send, part_recv, part_total, part_land,
-    table_q, table_g, gate_sem, gate_recv, qkv_sem, qkv_recv, sum_sem, part_sem, load_sem, table_sem,
+    slot_ref, layer_ref, table_q, table_g, gate_sem, gate_recv, qkv_sem, qkv_recv, sum_sem, part_sem, load_sem, table_sem,
 ):
     me = lax.axis_index("dev")
     grp = lax.axis_index("grp")
-
-    load_tq = pltpu.make_async_copy(stored_q, table_q, table_sem.at[1])
-    load_tg = pltpu.make_async_copy(stored_g, table_g, table_sem.at[2])
-
-    def load_head(head, _):
-        column = pl.ds(pl.multiple_of(head * HEAD_DIM, HEAD_DIM), HEAD_DIM)
-        pltpu.make_async_copy(qkv.at[:, :, column], qkv_in.at[head], table_sem.at[0]).start()
-        return 0
-
-    lax.fori_loop(0, NHEAD, load_head, 0)
-    load_tq.start()
-    load_tg.start()
 
     barrier = pltpu.get_barrier_semaphore()
 
@@ -119,6 +108,23 @@
             gate_recv.at[me],
         ).start()
 
+    fetches = [
+        pltpu.make_async_copy(source, target, table_sem.at[1 + i])
+        for i, (source, target) in enumerate(
+            ((head_slot, slot_ref), (layer_ids, layer_ref), (stored_q, table_q), (stored_g, table_g))
+        )
+    ]
+    for fetch in fetches:
+        fetch.start()
+
+    def load_head(head, _):
+        column = pl.ds(pl.multiple_of(head * HEAD_DIM, HEAD_DIM), HEAD_DIM)
+        pltpu.make_async_copy(qkv.at[:, :, column], qkv_in.at[head], table_sem.at[0]).start()
+        return 0
+
+    lax.fori_loop(0, NHEAD, load_head, 0)
+    for fetch in fetches:
+        fetch.wait()
     pltpu.make_async_copy(qkv_in, qkv_in, table_sem.at[0]).wait()
 
     def place(slot, _):
@@ -202,8 +208,6 @@
     sum_recv[me] = sum_send[me]
     qkv_land[own_rows] = qkv_send[me]
 
-    load_tq.wait()
-    load_tg.wait()
     row_of = lax.broadcasted_iota(jnp.int32, (8, STORED), 0)
     layer_of = lax.broadcasted_iota(jnp.int32, (8, STORED), 1)
     wanted = jnp.where(row_of == 0, layer_ref[0], layer_ref[1])
@@ -286,6 +290,11 @@
     parts = pl.ds(1, N_GRP - 1)
     from_others = part_recv.at[parts]
 
+    def give(total):
+        difference = total - expected[:LAYERS]
+        gate_mismatch[...] = difference[:, : 2 * BLOCKS]
+        qkv_mismatch[...] = difference[:, 2 * BLOCKS : 2 * BLOCKS + SLOTS]
+
     def total_to(k):
         return pltpu.make_async_remote_copy(
             src_ref=part_total,
@@ -302,7 +311,7 @@
         pltpu.make_async_copy(from_others, from_others, part_sem.at[1]).wait()
         total = jnp.sum(part_recv[...], axis=0)
         part_total[...] = total
-        mismatch[...] = total - expected[:LAYERS]
+        give(total)
         for k in range(1, N_GRP):
             total_to(k).start()
 
@@ -312,7 +321,7 @@
     @pl.when(grp > 0)
     def _():
         pltpu.make_async_copy(part_land, part_land, part_sem.at[3]).wait()
-        mismatch[...] = part_land[...] - expected[:LAYERS]
+        give(part_land[...])
         to_first.wait_send()
 
     @pl.when(grp == 0)
@@ -325,20 +334,35 @@
     pltpu.make_async_copy(gate_land.at[moved], gate_land.at[moved], gate_sem).wait()
 
 
+def put_out(gate, qkv, qkv_mismatch, gate_mismatch, gate_out, qkv_out, qkv_m_out, gate_m_out, sem):
+    height = N_DEV * ROWS // PIECES
+    pairs = [
+        (gate.at[layer, pl.ds(k * height, height)], gate_out.at[layer, pl.ds(k * height, height)])
+        for layer in range(LAYERS)
+        for k in range(PIECES)
+    ]
+    pairs += [(qkv, qkv_out), (qkv_mismatch, qkv_m_out), (gate_mismatch, gate_m_out)]
+    copies = [pltpu.make_async_copy(a, b, sem.at[i]) for i, (a, b) in enumerate(pairs)]
+    for copy in copies:
+        copy.start()
+    for copy in copies:
+        copy.wait()
+
+
 def body(qkv_weight, gate_up_weight, head_slot, layer_ids, stored_qkv, stored_gate_up):
     anywhere = pl.BlockSpec(memory_space=pl.ANY)
-    scalars = pl.BlockSpec(memory_space=pltpu.SMEM)
     in_vmem = pl.BlockSpec(memory_space=pltpu.VMEM)
     total_rows = N_DEV * ROWS
-    gate, qkv, mismatch = pl.pallas_call(
+    landed = pl.pallas_call(
         kernel,
         out_shape=(
             pltpu.VMEM((LAYERS, total_rows, 2 * WIDTH), jnp.bfloat16),
             pltpu.VMEM((LAYERS, total_rows, QW), jnp.bfloat16),
-            pltpu.VMEM((LAYERS, 128), jnp.float32),
+            pltpu.VMEM((LAYERS, SLOTS), jnp.float32),
+            pltpu.VMEM((LAYERS, 2 * BLOCKS), jnp.float32),
         ),
-        in_specs=[anywhere, anywhere, scalars, scalars, anywhere, anywhere],
-        out_specs=(in_vmem, in_vmem, in_vmem),
+        in_specs=[anywhere] * 6,
+        out_specs=(in_vmem,) * 4,
         scratch_shapes=[
             pltpu.VMEM((total_rows, LAYERS, 2 * WIDTH), jnp.bfloat16),
             pltpu.VMEM((total_rows, LAYERS, QW), jnp.bfloat16),
@@ -351,6 +375,8 @@
             pltpu.VMEM((N_GRP, LAYERS, 128), jnp.float32),
             pltpu.VMEM((LAYERS, 128), jnp.float32),
             pltpu.VMEM((LAYERS, 128), jnp.float32),
+            pltpu.SMEM((NHEAD,), jnp.int32),
+            pltpu.SMEM((LAYERS,), jnp.int32),
             pltpu.VMEM((STORED, NHEAD), jnp.int32),
             pltpu.VMEM((STORED, 2 * FF // BLK), jnp.int32),
             pltpu.SemaphoreType.DMA,
@@ -360,7 +386,7 @@
             pltpu.SemaphoreType.DMA((2,)),
             pltpu.SemaphoreType.DMA((4,)),
             pltpu.SemaphoreType.DMA((2, 2)),
-            pltpu.SemaphoreType.DMA((3,)),
+            pltpu.SemaphoreType.DMA((5,)),
         ],
         compiler_params=pltpu.CompilerParams(
             collective_id=0, has_side_effects=True, vmem_limit_bytes=50 << 20
@@ -374,12 +400,16 @@
         stored_qkv,
         stored_gate_up,
     )
-    return (
-        qkv,
-        gate,
-        mismatch[:, 2 * BLOCKS : 2 * BLOCKS + SLOTS],
-        mismatch[:, : 2 * BLOCKS],
-    )
+    served_gate, served_qkv, qkv_mismatch, gate_mismatch = pl.pallas_call(
+        put_out,
+        out_shape=tuple(jax.ShapeDtypeStruct(a.shape, a.dtype) for a in landed),
+        in_specs=[in_vmem] * 4,
+        out_specs=(anywhere,) * 4,
+        scratch_shapes=[pltpu.SemaphoreType.DMA((LAYERS * PIECES + 3,))],
+        compiler_params=pltpu.CompilerParams(vmem_limit_bytes=1 << 20),
+        name="put_out",
+    )(*landed)
+    return served_qkv, served_gate, qkv_mismatch, gate_mismatch
 
 
 def solution(mesh):

time: 150 us -> 146 us (0.973)
  local copies, waits for them, and re-layouts: 6.34 us -> 0 us
  Pallas kernels: 140 us -> 144 us
    unnamed x3 -> x0, local copies, waits for them, and re-layouts: 5.71 us -> none
    pallas_call x0 -> x1, Pallas kernels: none -> 4.46 us  [body(): pl.pallas_call(put_out, out_shape=tuple((jax.ShapeDtypeStruct(a.shape, a....]
where the time goes in v3:
time: 146 us; the launch traced here: 144 us
  Pallas kernels  144 us (99%)
    pallas_call x1, Pallas kernels, body(): pl.pallas_call(kernel, out_shape=(pltpu.VMEM((LAYERS, total_rows, 2 * WID...  139 us
    pallas_call x1, Pallas kernels, body(): pl.pallas_call(put_out, out_shape=tuple((jax.ShapeDtypeStruct(a.shape, a....  4.46 us

profile of v3, /device:TPU:40, one launch (start us, length us, event | category | flops | bytes accessed | tf_op | source)
XLA Modules:
  0.0 144.2 jit_solution(854438555198920604)
XLA Ops:
  0.6 139.1 %exchange.1 = (bf16[2,1152,2304]{2,1,0:T(8,128)(2,1)S(1)}, bf16[2,1152,256]{2,1,0:T(8,128)(2,1)S(1)}, f32[2,2]{1,0:T(2,128)S(1)}, f32[2,18]{1,0:T(2,128)S(1)}) custom-call(bf16[36,2,73728]{2,1,0:T(2,128)(2,1)} %bitcast.2, bf16[36,2,8192]{2,1,0:T(2,128)(2,1)} %bitcast.3, s32[64]{0:T(128)} %head_slot.1, s32[2]{0:T(128)} %layer_ids.1, s32[46,64]{1,0:T(8,128)} %stored_q.1, ...), custom_call_target="tpu_custom_call" | custom-call | tf_op jit(solution)/shard_map/exchange/pallas_call | solution.py:356
  139.8 4.5 %put_out.1 = (bf16[2,1152,2304]{2,1,0:T(8,128)(2,1)}, bf16[2,1152,256]{2,1,0:T(8,128)(2,1)}, f32[2,2]{1,0:T(2,128)}, f32[2,18]{1,0:T(2,128)}) custom-call(bf16[2,1152,2304]{2,1,0:T(8,128)(2,1)S(1)} %get-tuple-element.12.gate, bf16[2,1152,256]{2,1,0:T(8,128)(2,1)S(1)} %get-tuple-element.13.qkv, f32[2,2]{1,0:T(2,128)S(1)} %get-tuple-element.14.qkv_mismatch, ...), custom_call_target="tpu_custom_call" | custom-call | tf_op jit(solution)/shard_map/put_out/pallas_call | solution.py:403

commit v4 on v3

--- a/solution.py
+++ b/solution.py
@@ -27,9 +27,13 @@
 
 FAR_X = ((2, 1, 0, 1), (0, 1, 0, 1), (2, -1, 0, 1), (0, -1, 0, 1))
 FAR_Y = ((1, 2, 1, 0), (-1, 0, 1, 0), (-1, 2, 1, 0), (1, 0, 1, 0))
-DIAGONAL = ((1, 1, 1, 0), (-1, -1, 1, 0), (1, -1, 1, 0), (-1, 1, 1, 0))
+DIAGONAL = ((1, 1, 0, 0), (-1, -1, 0, 0))
+ANTIDIAGONAL = ((1, -1, 0, 0), (-1, 1, 0, 0))
 OPPOSITE = ((2, 0, 0, 0), (0, 2, 0, 0), (2, 2, 0, 0))
-ROUNDS = (FAR_X, OPPOSITE, FAR_Y, DIAGONAL)
+ROUNDS = (FAR_X, OPPOSITE, FAR_Y, DIAGONAL, ANTIDIAGONAL)
+
+
+FAR_FIRST = sorted(range(1, N_DEV), key=lambda k: -(min(k // 8, 4 - k // 8) + min(k // 2 % 4, 4 - k // 2 % 4)))
 
 
 def owner_at(me, offset, flip):
@@ -53,11 +57,8 @@
 
     barrier = pltpu.get_barrier_semaphore()
 
-    def greet(k, _):
+    for k in FAR_FIRST:
         pl.semaphore_signal(barrier, inc=1, device_id={"dev": (me + k) % N_DEV}, device_id_type=MESH)
-        return 0
-
-    lax.fori_loop(1, N_DEV, greet, 0)
 
     def greet_later(k, _):
         pl.semaphore_signal(barrier, inc=1, device_id={"grp": k}, device_id_type=MESH)
@@ -73,7 +74,7 @@
             src_ref=gate.at[:, :, pl.ds(pl.multiple_of(p * FF + owner * WIDTH, BLK), WIDTH)],
             dst_ref=gate_land.at[own_rows, :, pl.ds(pl.multiple_of(p * WIDTH, BLK), WIDTH)],
             send_sem=gate_sem,
-            recv_sem=gate_recv.at[me],
+            recv_sem=gate_recv.at[me, p],
             device_id={"dev": owner},
             device_id_type=MESH,
         ).start()
@@ -105,7 +106,7 @@
         pltpu.make_async_copy(
             gate.at[:, :, pl.ds(pl.multiple_of(p * FF + me * WIDTH, BLK), WIDTH)],
             gate_land.at[own_rows, :, pl.ds(p * WIDTH, WIDTH)],
-            gate_recv.at[me],
+            gate_recv.at[me, p],
         ).start()
 
     fetches = [
@@ -204,6 +205,7 @@
     lax.fori_loop(0, 2, qkv_sends, 0)
     gate_round(ROUNDS[2])
     gate_round(ROUNDS[3])
+    gate_round(ROUNDS[4])
 
     sum_recv[me] = sum_send[me]
     qkv_land[own_rows] = qkv_send[me]
@@ -240,27 +242,34 @@
             for layer in range(LAYERS):
                 out[layer, pl.ds(pl.multiple_of(start + 8 * i, 8), 8), column] = rows[i, layer]
 
-    def settle(land, out, landed, width, offset, only=None):
+    def chip_at(offset):
         x, y = me // 8, (me // 2) % 4
-        chip = (x + offset[0] + 4) % 4 * 4 + (y + offset[1] + 4) % 4
+        return (x + offset[0] + 4) % 4 * 4 + (y + offset[1] + 4) % 4
+
+    def settle(land, out, chip, first, width):
+        def step(i, _):
+            take_apart(land, out, chip, pl.ds(pl.multiple_of(first + i * BLK, BLK), BLK))
+            return 0
+
+        lax.fori_loop(0, width // BLK, step, 0)
+
+    def settle_gate(offsets):
+        for p in range(2):
+            for offset in offsets:
+                chip = chip_at(offset)
+                for core in range(2):
+                    source = chip * 2 + core
+                    block = gate_land.at[pl.ds(source * ROWS, ROWS), :, pl.ds(p * WIDTH, WIDTH)]
+                    pltpu.make_async_copy(block, block, gate_recv.at[source, p]).wait()
+                settle(gate_land, gate_out, chip, p * WIDTH, WIDTH)
+
+    def settle_qkv(offset):
+        chip = chip_at(offset)
         for core in range(2):
             source = chip * 2 + core
-            block = land.at[pl.ds(source * ROWS, ROWS)]
-            wait = pltpu.make_async_copy(block, block, landed.at[source]).wait
-            if only is None:
-                wait()
-            else:
-                pl.when(source != me)(wait)
-
-        def step(i, _):
-            take_apart(land, out, chip, pl.ds(pl.multiple_of(i * BLK, BLK), BLK))
-            return 0
-
-        lax.fori_loop(0, width // BLK, step, 0)
-
-    def settle_gate(offsets):
-        for offset in offsets:
-            settle(gate_land, gate_out, gate_recv, 2 * WIDTH, offset)
+            block = qkv_land.at[pl.ds(source * ROWS, ROWS)]
+            pl.when(source != me)(pltpu.make_async_copy(block, block, qkv_recv.at[source]).wait)
+        settle(qkv_land, qkv_out, chip, 0, QW)
 
     here = ((0, 0),)
     settle_gate(here)
@@ -283,10 +292,9 @@
     def _():
         to_first.start()
 
-    settle(qkv_land, qkv_out, qkv_recv, QW, here[0], only="others")
-    for offsets in ROUNDS:
+    for offsets in (here,) + ROUNDS:
         for offset in offsets:
-            settle(qkv_land, qkv_out, qkv_recv, QW, offset)
+            settle_qkv(offset)
     parts = pl.ds(1, N_GRP - 1)
     from_others = part_recv.at[parts]
 
@@ -317,6 +325,7 @@
 
     settle_gate(ROUNDS[2])
     settle_gate(ROUNDS[3])
+    settle_gate(ROUNDS[4])
 
     @pl.when(grp > 0)
     def _():
@@ -380,7 +389,7 @@
             pltpu.VMEM((STORED, NHEAD), jnp.int32),
             pltpu.VMEM((STORED, 2 * FF // BLK), jnp.int32),
             pltpu.SemaphoreType.DMA,
-            pltpu.SemaphoreType.DMA((N_DEV,)),
+            pltpu.SemaphoreType.DMA((N_DEV, 2)),
             pltpu.SemaphoreType.DMA,
             pltpu.SemaphoreType.DMA((N_DEV,)),
             pltpu.SemaphoreType.DMA((2,)),

time: 146 us -> 145 us (level)
  the two profiles are of different devices: /device:TPU:40 before, /device:TPU:1 now
where the time goes in v4:
time: 145 us; the launch traced here: 144 us
  Pallas kernels  143 us (99%)
    pallas_call x1, Pallas kernels, body(): pl.pallas_call(kernel, out_shape=(pltpu.VMEM((LAYERS, total_rows, 2 * WID...  139 us
    pallas_call x1, Pallas kernels, body(): pl.pallas_call(put_out, out_shape=tuple((jax.ShapeDtypeStruct(a.shape, a....  4.46 us

profile of v4, /device:TPU:1, one launch (start us, length us, event | category | flops | bytes accessed | tf_op | source)
XLA Modules:
  0.0 143.9 jit_solution(4018729777395523762)
XLA Ops:
  0.6 138.8 %exchange.1 = (bf16[2,1152,2304]{2,1,0:T(8,128)(2,1)S(1)}, bf16[2,1152,256]{2,1,0:T(8,128)(2,1)S(1)}, f32[2,2]{1,0:T(2,128)S(1)}, f32[2,18]{1,0:T(2,128)S(1)}) custom-call(bf16[36,2,73728]{2,1,0:T(2,128)(2,1)} %bitcast.2, bf16[36,2,8192]{2,1,0:T(2,128)(2,1)} %bitcast.3, s32[64]{0:T(128)} %head_slot.1, s32[2]{0:T(128)} %layer_ids.1, s32[46,64]{1,0:T(8,128)} %stored_q.1, ...), custom_call_target="tpu_custom_call" | custom-call | tf_op jit(solution)/shard_map/exchange/pallas_call | solution.py:365
  139.5 4.5 %put_out.1 = (bf16[2,1152,2304]{2,1,0:T(8,128)(2,1)}, bf16[2,1152,256]{2,1,0:T(8,128)(2,1)}, f32[2,2]{1,0:T(2,128)}, f32[2,18]{1,0:T(2,128)}) custom-call(bf16[2,1152,2304]{2,1,0:T(8,128)(2,1)S(1)} %get-tuple-element.12.gate, bf16[2,1152,256]{2,1,0:T(8,128)(2,1)S(1)} %get-tuple-element.13.qkv, f32[2,2]{1,0:T(2,128)S(1)} %get-tuple-element.14.qkv_mismatch, ...), custom_call_target="tpu_custom_call" | custom-call | tf_op jit(solution)/shard_map/put_out/pallas_call | solution.py:412

commit v5 on v4

--- a/solution.py
+++ b/solution.py
@@ -21,6 +21,8 @@
 SLOTS = NHEAD // N_DEV
 QW = SLOTS * HEAD_DIM
 PIECES = 4
+CHIP_ROWS = 2 * ROWS
+VMEM_LIMIT = 38
 
 stored_unit = 1.0 / 1024.0
 MESH = pl.DeviceIdType.MESH
@@ -31,6 +33,7 @@
 ANTIDIAGONAL = ((1, -1, 0, 0), (-1, 1, 0, 0))
 OPPOSITE = ((2, 0, 0, 0), (0, 2, 0, 0), (2, 2, 0, 0))
 ROUNDS = (FAR_X, OPPOSITE, FAR_Y, DIAGONAL, ANTIDIAGONAL)
+LAST = DIAGONAL + ANTIDIAGONAL
 
 
 FAR_FIRST = sorted(range(1, N_DEV), key=lambda k: -(min(k // 8, 4 - k // 8) + min(k // 2 % 4, 4 - k // 2 % 4)))
@@ -47,8 +50,8 @@
 
 def kernel(
     gate, qkv, head_slot, layer_ids, stored_q, stored_g,
-    gate_out, qkv_out, qkv_mismatch, gate_mismatch,
-    gate_land, qkv_land,
+    gate_out, gate_land, qkv_out, qkv_mismatch, gate_mismatch,
+    qkv_land,
     qkv_in, qkv_send, rows_in, sum_send, sum_recv, part_send, part_recv, part_total, part_land,
     slot_ref, layer_ref, table_q, table_g, gate_sem, gate_recv, qkv_sem, qkv_recv, sum_sem, part_sem, load_sem, table_sem,
 ):
@@ -194,7 +197,6 @@
         ).start()
         return 0
 
-    lax.fori_loop(1, N_DEV, small_sends, 0)
     send_qkv(partner)
 
     def qkv_sends(flip, _):
@@ -203,6 +205,7 @@
         return 0
 
     lax.fori_loop(0, 2, qkv_sends, 0)
+    lax.fori_loop(1, N_DEV, small_sends, 0)
     gate_round(ROUNDS[2])
     gate_round(ROUNDS[3])
     gate_round(ROUNDS[4])
@@ -234,37 +237,30 @@
         pick_q = jnp.where(hit, 1.0, pick_q)
     expected = (picked(table_g[...], pick_g) + picked(table_q[...], pick_q)) * stored_unit
 
-    def take_apart(land, out, chip, column):
-        start = pl.multiple_of(chip * 2 * ROWS, 8)
-        rows = land[pl.ds(start, 2 * ROWS), :, column].reshape(2 * ROWS // 8, 8, LAYERS, BLK)
-        rows = jnp.swapaxes(rows, 1, 2)
-        for i in range(2 * ROWS // 8):
-            for layer in range(LAYERS):
-                out[layer, pl.ds(pl.multiple_of(start + 8 * i, 8), 8), column] = rows[i, layer]
-
-    def chip_at(offset):
-        x, y = me // 8, (me // 2) % 4
-        return (x + offset[0] + 4) % 4 * 4 + (y + offset[1] + 4) % 4
-
     def settle(land, out, chip, first, width):
         def step(i, _):
-            take_apart(land, out, chip, pl.ds(pl.multiple_of(first + i * BLK, BLK), BLK))
+            column = pl.ds(pl.multiple_of(first + i * BLK, BLK), BLK)
+            rows = take_apart(land, chip, column)
+            for k in range(CHIP_ROWS // 8):
+                for layer in range(LAYERS):
+                    out[layer, pl.ds(pl.multiple_of(chip * CHIP_ROWS + 8 * k, 8), 8), column] = rows[k, layer]
             return 0
 
         lax.fori_loop(0, width // BLK, step, 0)
 
-    def settle_gate(offsets):
+    def settle_gate(offsets, last=False):
         for p in range(2):
             for offset in offsets:
-                chip = chip_at(offset)
+                chip = chip_at(me, offset)
                 for core in range(2):
                     source = chip * 2 + core
                     block = gate_land.at[pl.ds(source * ROWS, ROWS), :, pl.ds(p * WIDTH, WIDTH)]
                     pltpu.make_async_copy(block, block, gate_recv.at[source, p]).wait()
-                settle(gate_land, gate_out, chip, p * WIDTH, WIDTH)
+                if not (last and p):
+                    settle(gate_land, gate_out, chip, p * WIDTH, WIDTH)
 
     def settle_qkv(offset):
-        chip = chip_at(offset)
+        chip = chip_at(me, offset)
         for core in range(2):
             source = chip * 2 + core
             block = qkv_land.at[pl.ds(source * ROWS, ROWS)]
@@ -288,11 +284,14 @@
         device_id_type=MESH,
     )
 
+    for offset in here + ROUNDS[0]:
+        settle_qkv(offset)
+
     @pl.when(grp > 0)
     def _():
         to_first.start()
 
-    for offsets in (here,) + ROUNDS:
+    for offsets in ROUNDS[1:]:
         for offset in offsets:
             settle_qkv(offset)
     parts = pl.ds(1, N_GRP - 1)
@@ -320,12 +319,14 @@
         total = jnp.sum(part_recv[...], axis=0)
         part_total[...] = total
         give(total)
+    settle_gate(ROUNDS[2])
+
+    @pl.when(grp == 0)
+    def _():
         for k in range(1, N_GRP):
             total_to(k).start()
 
-    settle_gate(ROUNDS[2])
-    settle_gate(ROUNDS[3])
-    settle_gate(ROUNDS[4])
+    settle_gate(LAST, last=True)
 
     @pl.when(grp > 0)
     def _():
@@ -343,19 +344,74 @@
     pltpu.make_async_copy(gate_land.at[moved], gate_land.at[moved], gate_sem).wait()
 
 
-def put_out(gate, qkv, qkv_mismatch, gate_mismatch, gate_out, qkv_out, qkv_m_out, gate_m_out, sem):
+def take_apart(land, chip, column):
+    rows = land[pl.ds(pl.multiple_of(chip * CHIP_ROWS, 8), CHIP_ROWS), :, column]
+    return jnp.swapaxes(rows.reshape(CHIP_ROWS // 8, 8, LAYERS, BLK), 1, 2)
+
+
+def chip_at(me, offset):
+    x, y = me // 8, (me // 2) % 4
+    return (x + offset[0] + 4) % 4 * 4 + (y + offset[1] + 4) % 4
+
+
+def put_out(gate, land, qkv, qkv_mismatch, gate_mismatch, gate_out, qkv_out, qkv_m_out, gate_m_out, rest, sem):
+    me = lax.axis_index("dev")
+    gate_columns, up_columns = pl.ds(0, WIDTH), pl.ds(WIDTH, WIDTH)
+    last = [chip_at(me, offset) for offset in LAST]
     height = N_DEV * ROWS // PIECES
-    pairs = [
-        (gate.at[layer, pl.ds(k * height, height)], gate_out.at[layer, pl.ds(k * height, height)])
+    copies = [
+        pltpu.make_async_copy(
+            gate.at[layer, pl.ds(k * height, height), gate_columns],
+            gate_out.at[layer, pl.ds(k * height, height), gate_columns],
+            sem.at[layer * PIECES + k],
+        )
         for layer in range(LAYERS)
         for k in range(PIECES)
     ]
-    pairs += [(qkv, qkv_out), (qkv_mismatch, qkv_m_out), (gate_mismatch, gate_m_out)]
-    copies = [pltpu.make_async_copy(a, b, sem.at[i]) for i, (a, b) in enumerate(pairs)]
+    small = ((qkv, qkv_out), (qkv_mismatch, qkv_m_out), (gate_mismatch, gate_m_out))
+    copies += [pltpu.make_async_copy(a, b, sem.at[LAYERS * PIECES + i]) for i, (a, b) in enumerate(small)]
+    first_up = len(copies)
+
+    def up(chip, source):
+        rows = pl.ds(pl.multiple_of(chip * CHIP_ROWS, 8), CHIP_ROWS)
+        target = gate_out.at[:, rows, up_columns]
+        return pltpu.make_async_copy(
+            gate.at[:, rows, up_columns] if source is None else source, target, sem.at[first_up + chip]
+        )
+
     for copy in copies:
         copy.start()
+
+    def start_up(chip, _):
+        left = (chip != last[0]) & (chip != last[1]) & (chip != last[2]) & (chip != last[3])
+
+        @pl.when(left)
+        def _():
+            up(chip, None).start()
+
+        return 0
+
+    lax.fori_loop(0, N_DEV // 2, start_up, 0)
+    for at, chip in enumerate(last):
+
+        def step(i, _):
+            rows = take_apart(land, chip, pl.ds(pl.multiple_of(WIDTH + i * BLK, BLK), BLK))
+            for k in range(CHIP_ROWS // 8):
+                for layer in range(LAYERS):
+                    rest[at, layer, pl.ds(8 * k, 8), pl.ds(pl.multiple_of(i * BLK, BLK), BLK)] = rows[k, layer]
+            return 0
+
+        lax.fori_loop(0, BLOCKS, step, 0)
+    for at, chip in enumerate(last):
+        up(chip, rest.at[at]).start()
     for copy in copies:
         copy.wait()
+
+    def end_up(chip, _):
+        up(chip, None).wait()
+        return 0
+
+    lax.fori_loop(0, N_DEV // 2, end_up, 0)
 
 
 def body(qkv_weight, gate_up_weight, head_slot, layer_ids, stored_qkv, stored_gate_up):
@@ -366,14 +422,14 @@
         kernel,
         out_shape=(
             pltpu.VMEM((LAYERS, total_rows, 2 * WIDTH), jnp.bfloat16),
+            pltpu.VMEM((total_rows, LAYERS, 2 * WIDTH), jnp.bfloat16),
             pltpu.VMEM((LAYERS, total_rows, QW), jnp.bfloat16),
             pltpu.VMEM((LAYERS, SLOTS), jnp.float32),
             pltpu.VMEM((LAYERS, 2 * BLOCKS), jnp.float32),
         ),
         in_specs=[anywhere] * 6,
-        out_specs=(in_vmem,) * 4,
+        out_specs=(in_vmem,) * 5,
         scratch_shapes=[
-            pltpu.VMEM((total_rows, LAYERS, 2 * WIDTH), jnp.bfloat16),
             pltpu.VMEM((total_rows, LAYERS, QW), jnp.bfloat16),
             pltpu.VMEM((NHEAD, ROWS, LAYERS, HEAD_DIM), jnp.bfloat16),
             pltpu.VMEM((N_DEV, ROWS, LAYERS, QW), jnp.bfloat16),
@@ -398,7 +454,7 @@
             pltpu.SemaphoreType.DMA((5,)),
         ],
         compiler_params=pltpu.CompilerParams(
-            collective_id=0, has_side_effects=True, vmem_limit_bytes=50 << 20
+            collective_id=0, has_side_effects=True, vmem_limit_bytes=VMEM_LIMIT << 20
         ),
         name="exchange",
     )(
@@ -411,11 +467,14 @@
     )
     served_gate, served_qkv, qkv_mismatch, gate_mismatch = pl.pallas_call(
         put_out,
-        out_shape=tuple(jax.ShapeDtypeStruct(a.shape, a.dtype) for a in landed),
-        in_specs=[in_vmem] * 4,
+        out_shape=tuple(jax.ShapeDtypeStruct(a.shape, a.dtype) for a in landed[:1] + landed[2:]),
+        in_specs=[in_vmem] * 5,
         out_specs=(anywhere,) * 4,
-        scratch_shapes=[pltpu.SemaphoreType.DMA((LAYERS * PIECES + 3,))],
-        compiler_params=pltpu.CompilerParams(vmem_limit_bytes=1 << 20),
+        scratch_shapes=[
+            pltpu.VMEM((len(LAST), LAYERS, CHIP_ROWS, WIDTH), jnp.bfloat16),
+            pltpu.SemaphoreType.DMA((LAYERS * PIECES + 3 + N_DEV // 2,)),
+        ],
+        compiler_params=pltpu.CompilerParams(vmem_limit_bytes=8 << 20),
         name="put_out",
     )(*landed)
     return served_qkv, served_gate, qkv_mismatch, gate_mismatch

time: 145 us -> 144 us (level)
  the two profiles are of different devices: /device:TPU:1 before, /device:TPU:40 now
where the time goes in v5:
time: 144 us; the launch traced here: 141 us
  Pallas kernels  141 us (98%)
    pallas_call x1, Pallas kernels, body(): pl.pallas_call(kernel, out_shape=(pltpu.VMEM((LAYERS, total_rows, 2 * WID...  136 us
    pallas_call x1, Pallas kernels, body(): pl.pallas_call(put_out, out_shape=tuple((jax.ShapeDtypeStruct(a.shape, a....  4.55 us

profile of v5, /device:TPU:40, one launch (start us, length us, event | category | flops | bytes accessed | tf_op | source)
XLA Modules:
  0.0 141.2 jit_solution(14411005412827229968)
XLA Ops:
  0.6 136.0 %exchange.1 = (bf16[2,1152,2304]{2,1,0:T(8,128)(2,1)S(1)}, bf16[1152,2,2304]{2,1,0:T(2,128)(2,1)S(1)}, bf16[2,1152,256]{2,1,0:T(8,128)(2,1)S(1)}, f32[2,2]{1,0:T(2,128)S(1)}, f32[2,18]{1,0:T(2,128)S(1)}) custom-call(bf16[36,2,73728]{2,1,0:T(2,128)(2,1)} %bitcast.2, bf16[36,2,8192]{2,1,0:T(2,128)(2,1)} %bitcast.3, s32[64]{0:T(128)} %head_slot.1, s32[2]{0:T(128)} %layer_ids.1, ...), custom_call_target="tpu_custom_call" | custom-call | tf_op jit(solution)/shard_map/exchange/pallas_call | solution.py:421
  136.6 4.6 %put_out.1 = (bf16[2,1152,2304]{2,1,0:T(8,128)(2,1)}, bf16[2,1152,256]{2,1,0:T(8,128)(2,1)}, f32[2,2]{1,0:T(2,128)}, f32[2,18]{1,0:T(2,128)}) custom-call(bf16[2,1152,2304]{2,1,0:T(8,128)(2,1)S(1)} %get-tuple-element.13.gate, bf16[1152,2,2304]{2,1,0:T(2,128)(2,1)S(1)} %get-tuple-element.14.land, bf16[2,1152,256]{2,1,0:T(8,128)(2,1)S(1)} %get-tuple-element.15.qkv, ...), custom_call_target="tpu_custom_call" | custom-call | tf_op jit(solution)/shard_map/put_out/pallas_call | solution.py:468

commit v6 on v5

--- a/solution.py
+++ b/solution.py
@@ -105,6 +105,7 @@
         send_gate(partner, p)
     gate_round(ROUNDS[0])
     gate_round(ROUNDS[1])
+    gate_round(ROUNDS[2])
     for p in range(2):
         pltpu.make_async_copy(
             gate.at[:, :, pl.ds(pl.multiple_of(p * FF + me * WIDTH, BLK), WIDTH)],
@@ -206,7 +207,6 @@
 
     lax.fori_loop(0, 2, qkv_sends, 0)
     lax.fori_loop(1, N_DEV, small_sends, 0)
-    gate_round(ROUNDS[2])
     gate_round(ROUNDS[3])
     gate_round(ROUNDS[4])
 

time: 144 us -> 144 us (level)
  no operation moved by 1% of the time
where the time goes in v6:
time: 144 us; the launch traced here: 141 us
  Pallas kernels  140 us (97%)
    pallas_call x1, Pallas kernels, body(): pl.pallas_call(kernel, out_shape=(pltpu.VMEM((LAYERS, total_rows, 2 * WID...  136 us
    pallas_call x1, Pallas kernels, body(): pl.pallas_call(put_out, out_shape=tuple((jax.ShapeDtypeStruct(a.shape, a....  4.55 us

profile of v6, /device:TPU:40, one launch (start us, length us, event | category | flops | bytes accessed | tf_op | source)
XLA Modules:
  0.0 141.1 jit_solution(18337513845956863721)
XLA Ops:
  0.6 135.9 %exchange.1 = (bf16[2,1152,2304]{2,1,0:T(8,128)(2,1)S(1)}, bf16[1152,2,2304]{2,1,0:T(2,128)(2,1)S(1)}, bf16[2,1152,256]{2,1,0:T(8,128)(2,1)S(1)}, f32[2,2]{1,0:T(2,128)S(1)}, f32[2,18]{1,0:T(2,128)S(1)}) custom-call(bf16[36,2,73728]{2,1,0:T(2,128)(2,1)} %bitcast.2, bf16[36,2,8192]{2,1,0:T(2,128)(2,1)} %bitcast.3, s32[64]{0:T(128)} %head_slot.1, s32[2]{0:T(128)} %layer_ids.1, ...), custom_call_target="tpu_custom_call" | custom-call | tf_op jit(solution)/shard_map/exchange/pallas_call | solution.py:421
  136.5 4.6 %put_out.1 = (bf16[2,1152,2304]{2,1,0:T(8,128)(2,1)}, bf16[2,1152,256]{2,1,0:T(8,128)(2,1)}, f32[2,2]{1,0:T(2,128)}, f32[2,18]{1,0:T(2,128)}) custom-call(bf16[2,1152,2304]{2,1,0:T(8,128)(2,1)S(1)} %get-tuple-element.13.gate, bf16[1152,2,2304]{2,1,0:T(2,128)(2,1)S(1)} %get-tuple-element.14.land, bf16[2,1152,256]{2,1,0:T(8,128)(2,1)S(1)} %get-tuple-element.15.qkv, ...), custom_call_target="tpu_custom_call" | custom-call | tf_op jit(solution)/shard_map/put_out/pallas_call | solution.py:468
